TPU v7x, 32 devices: a whole 2x2x4 slice. The times are simulated.
32 devices in a mesh: grp: 8 (over y, x, core), rng: 4 (over z).
Axes of the slice: x: 2, y: 2, z: 4, core: 2. Of those that a mesh axis runs over, the one named last changes fastest.
Arguments:
- features: bfloat16 [8192, 1024], P(('grp', 'rng')), may hold values from -6 to 6
- query_weight: bfloat16 [1024, 1024], replicated
- key_weight: bfloat16 [1024, 1024], replicated
- value_weight: bfloat16 [1024, 1024], replicated, may hold values from -0.1875 to 0.1875
- out_weight: bfloat16 [1024, 1024], replicated, may hold values from -0.1875 to 0.1875
- band_reach: int32 [32], P(('grp', 'rng')), may hold values from 16 to 128, as said below
- long_peers: int32 [64, 6], P(('grp', 'rng')), may hold values from 0 to 7, as said below
- long_count: int32 [64], P(('grp', 'rng')), may hold values from 0 to 6, as said below
- send_tile: int32 [32, 8], P(('grp', 'rng')), may hold values from 0 to 3
Outputs:
- updated: bfloat16 [8192, 1024], P(('grp', 'rng'))
Inputs may be any that keep to these rules, and one draw needn't show every extreme that they name: `band_reach`: some range has 128 in every draw. `long_peers`: the 6 entries of a query tile in region g are distinct regions other than g; only the first long_count entries are used. `long_count`: some query tile has 6 in every draw.
All inputs are finite; a program needn't handle non-finite values.
Results may differ from a plain program's by a relative error of at most 0.0064.
Values may be sent and summed in bfloat16 or wider, within the bound.
A program may use at most 128 MiB of HBM per device.

v0:
```python
import functools

import jax
import jax.numpy as jnp
from jax import lax
from jax.experimental import pallas as pl
from jax.experimental.pallas import tpu as pltpu
from jax.sharding import PartitionSpec as P

HEADS = 16
TILE = 128
PORTAL = 64
EPSILON = 1e-06
LOG2E = 1.4426950408889634
MESH = pl.DeviceIdType.MESH
F32 = jnp.float32
BF16 = jnp.bfloat16


def flipped(index, offset):
    result = index
    bit = 1
    while bit <= offset:
        if offset & bit:
            result = result + bit * (1 - 2 * ((index // bit) % 2))
        bit *= 2
    return result


def rms_normed(rows):
    widened = rows.astype(F32)
    factor = lax.rsqrt(jnp.mean(widened * widened, axis=1, keepdims=True) + EPSILON)
    return (widened * factor).astype(BF16)


def nt_dot(lhs, rhs):
    return lax.dot_general(lhs, rhs, (((1,), (1,)), ((), ())), preferred_element_type=F32)


def kernel(
    n_grp,
    n_rng,
    early,
    late,
    feat_hbm,
    wq_hbm,
    wk_hbm,
    wv_hbm,
    wo_hbm,
    reach_ref,
    peers_ref,
    count_ref,
    pick_ref,
    out_ref,
    x_ref,
    wq,
    wk,
    wv,
    wo,
    stage,
    halo,
    port_e,
    port_t,
    q_s,
    xn_l,
    xn_e,
    xn_t,
    acc,
    top,
    att,
    bias_l,
    bias_h,
    bias_e,
    bias_t,
    load_sem,
    send_sem,
    recv_sem,
):
    rows, width = x_ref.shape
    tiles = rows // TILE
    head_dim = width // HEADS
    lanes = 2 * head_dim
    pairs = width // lanes
    grp = lax.axis_index("grp")
    rng = lax.axis_index("rng")
    loads = [
        pltpu.make_async_copy(src, dst, load_sem.at[i])
        for i, (src, dst) in enumerate(
            ((feat_hbm, x_ref), (wq_hbm, wq), (wk_hbm, wk), (wv_hbm, wv), (wo_hbm, wo))
        )
    ]
    loads[0].start()

    above = lax.rem(rng + 1, n_rng)
    below = lax.rem(rng + n_rng - 1, n_rng)
    barrier = pltpu.get_barrier_semaphore()
    for other in (above, below):
        pl.semaphore_signal(barrier, inc=1, device_id=(grp, other), device_id_type=MESH)
    for offset in range(1, n_grp):
        pl.semaphore_signal(
            barrier, inc=1, device_id=(flipped(grp, offset), rng), device_id_type=MESH
        )

    loads[0].wait()
    for load in loads[1:]:
        load.start()
    for offset in range(1, n_grp):
        pick = jnp.full((PORTAL, width), pick_ref[0, flipped(grp, offset)], jnp.int32)
        chosen = x_ref[0:PORTAL, :]
        for i in range(1, rows // PORTAL):
            chosen = jnp.where(pick == i, x_ref[i * PORTAL : (i + 1) * PORTAL, :], chosen)
        stage[offset - 1] = chosen
    pl.semaphore_wait(barrier, n_grp + 1)

    def remote(src, dst, slot, device):
        copy = pltpu.make_async_remote_copy(
            src_ref=src,
            dst_ref=dst,
            send_sem=send_sem.at[slot],
            recv_sem=recv_sem.at[slot],
            device_id=device,
            device_id_type=MESH,
        )
        copy.start()
        return copy

    halo_copies = [
        remote(x_ref.at[pl.ds(rows - TILE, TILE)], halo.at[0], 0, (grp, above)),
        remote(x_ref.at[pl.ds(0, TILE)], halo.at[1], 1, (grp, below)),
    ]

    def send_portals(offsets, buffer):
        return [
            remote(
                stage.at[offset - 1],
                buffer.at[pl.ds(i * PORTAL, PORTAL)],
                1 + offset,
                (flipped(grp, offset), rng),
            )
            for i, offset in enumerate(offsets)
        ]

    early_copies = send_portals(early, port_e)
    late_copies = send_portals(late, port_t)

    reach = reach_ref[0]
    row_pos = lax.broadcasted_iota(jnp.int32, (rows, rows), 0)
    key_pos = lax.broadcasted_iota(jnp.int32, (rows, rows), 1)
    bias_l[...] = jnp.where(jnp.abs(row_pos - key_pos) <= reach, 0.0, -jnp.inf)
    row_pos = lax.broadcasted_iota(jnp.int32, (TILE, TILE), 0)
    key_pos = lax.broadcasted_iota(jnp.int32, (TILE, TILE), 1)
    bias_h[0] = jnp.where(row_pos + TILE - key_pos <= reach, 0.0, -jnp.inf)
    bias_h[1] = jnp.where(key_pos + TILE - row_pos <= reach, 0.0, -jnp.inf)

    def portal_bias(offsets, bias_ref):
        place = lax.broadcasted_iota(jnp.int32, (1, len(offsets) * PORTAL), 1) // PORTAL
        for t in range(tiles):
            live = jnp.zeros(place.shape, jnp.int32)
            for i, offset in enumerate(offsets):
                source = flipped(grp, offset)
                listed = jnp.int32(0)
                for s in range(peers_ref.shape[1]):
                    used = jnp.logical_and(s < count_ref[t], peers_ref[t, s] == source)
                    listed = listed + used.astype(jnp.int32)
                live = jnp.where(place == i, listed, live)
            bias_ref[t] = jnp.where(live > 0, 0.0, -jnp.inf)

    portal_bias(early, bias_e)
    portal_bias(late, bias_t)

    scale = head_dim ** (-0.5) * LOG2E
    block = 2 * lanes

    def product(weights, values):
        return jnp.dot(weights.astype(BF16), values, preferred_element_type=F32)

    def projected(source, weight, part):
        return product(source[...], weight[:, part * block : (part + 1) * block])

    def keys_of(source, part):
        return projected(source, wk, part).astype(BF16)

    def values_of(source, part):
        return projected(source, wv, part).astype(BF16)

    def split_values(values):
        low = lax.broadcasted_iota(jnp.int32, values.shape, 1) < head_dim
        one = jnp.ones_like(values)
        return jnp.where(low, values, one), jnp.where(low, one, values)

    def widened(stat, count):
        whole, rest = count // lanes, count % lanes
        parts = [stat] * whole + ([stat[:, :rest]] if rest else [])
        return jnp.concatenate(parts, axis=1) if len(parts) > 1 else parts[0]

    def q_pair(pair, places=slice(None)):
        picked = q_s[:, places, pair * lanes : (pair + 1) * lanes]
        return picked.reshape(2 * picked.shape[1], lanes)

    def spread(bias_ref, count):
        return jnp.concatenate(
            [jnp.broadcast_to(bias_ref[t], (TILE, count)) for t in range(tiles)], axis=0
        )

    def stacked(*parts):
        return jnp.concatenate([part for part in parts if part.shape[0]], axis=0)

    def local_pair(pair, keys, values):
        value_pair = split_values(values)
        both = nt_dot(q_pair(pair), keys)
        for parity in range(2):
            scores = both[parity * rows : (parity + 1) * rows] + bias_l[...]
            highest = jnp.max(scores, axis=1, keepdims=True)
            acc[pair, parity] = product(jnp.exp2(scores - highest), value_pair[parity])
            top[pair, parity] = jnp.broadcast_to(highest, (rows, lanes))

    def early_pair(pair, keys, values):
        value_pair = split_values(values)
        both = nt_dot(q_pair(pair), keys)
        for parity in range(2):
            scores = both[parity * rows : (parity + 1) * rows] + spread(bias_e, keys.shape[0])
            before = top[pair, parity]
            highest = jnp.maximum(before, jnp.max(scores, axis=1, keepdims=True))
            weights = jnp.exp2(scores - widened(highest, scores.shape[1]))
            acc[pair, parity] = acc[pair, parity] * jnp.exp2(before - highest) + product(
                weights, value_pair[parity]
            )
            top[pair, parity] = highest

    def late_pair(pair, keys, values):
        value_pair = split_values(values[2 * TILE :])
        edges = []
        for side in range(2):
            span = slice(side * TILE, (side + 1) * TILE)
            place = slice(side * (rows - TILE), side * (rows - TILE) + TILE)
            edges.append((nt_dot(q_pair(pair, place), keys[span]), split_values(values[span])))
        both = nt_dot(q_pair(pair), keys[2 * TILE :])
        halves = []
        for parity in range(2):
            scores = both[parity * rows : (parity + 1) * rows]
            scores = scores + spread(bias_t, scores.shape[1])
            before = top[pair, parity]
            highest = jnp.maximum(before, jnp.max(scores, axis=1, keepdims=True))
            band = [
                edge[parity * TILE : (parity + 1) * TILE] + bias_h[side]
                for side, (edge, _) in enumerate(edges)
            ]
            sides = [jnp.max(part, axis=1, keepdims=True) for part in band]
            low = jnp.maximum(highest[:TILE], sides[0])
            high = jnp.maximum(highest[rows - TILE :], sides[1])
            highest = stacked(low, highest[TILE : rows - TILE], high)
            mixed = acc[pair, parity] * jnp.exp2(before - highest)
            weights = jnp.exp2(scores - widened(highest, scores.shape[1]))
            mixed = mixed + product(weights, value_pair[parity])
            low = mixed[:TILE] + product(jnp.exp2(band[0] - low), edges[0][1][parity])
            high = mixed[rows - TILE :] + product(jnp.exp2(band[1] - high), edges[1][1][parity])
            halves.append(stacked(low, mixed[TILE : rows - TILE], high))
        left = lax.broadcasted_iota(jnp.int32, (rows, lanes), 1) < head_dim
        even, odd = halves
        total = pltpu.roll(jnp.where(left, odd, even), head_dim, 1)
        att[:, pair * lanes : (pair + 1) * lanes] = (
            jnp.where(left, even, odd) / total
        ).astype(BF16)

    def local_queries(part):
        queries = (projected(xn_l, wq, part) * scale).astype(BF16)
        column = lax.broadcasted_iota(jnp.int32, queries.shape, 1)
        first = lax.rem(column, lanes) < head_dim
        zero = jnp.zeros_like(queries)
        cols = slice(part * block, (part + 1) * block)
        q_s[0, :, cols] = jnp.where(first, queries, zero)
        q_s[1, :, cols] = jnp.where(first, zero, queries)

    xn_l[...] = rms_normed(x_ref[...])
    loads[1].wait()
    for part in range(width // block):
        local_queries(part)
    loads[2].wait()
    loads[3].wait()

    def early_ready():
        for copy in early_copies:
            copy.wait_recv()
        xn_e[...] = rms_normed(port_e[...])

    def late_ready():
        for copy in halo_copies + late_copies:
            copy.wait_recv()
        xn_t[: 2 * TILE] = rms_normed(halo[...].reshape(2 * TILE, width))
        xn_t[2 * TILE :] = rms_normed(port_t[...])

    steps = []
    for source, ready, attend in (
        (xn_l, None, local_pair),
        (xn_e, early_ready, early_pair),
        (xn_t, late_ready, late_pair),
    ):
        for part in range(width // block):
            steps.append((source, ready if part == 0 else None, attend, part))
    keys = keys_of(xn_l, 0)
    values = values_of(xn_l, 0)
    for number, (_, _, attend, part) in enumerate(steps):
        follower = steps[number + 1] if number + 1 < len(steps) else None
        if follower is not None and follower[1] is not None:
            follower[1]()
        attend(2 * part, keys[:, :lanes], values[:, :lanes])
        if follower is not None:
            next_keys = keys_of(follower[0], follower[3])
        attend(2 * part + 1, keys[:, lanes:], values[:, lanes:])
        if follower is not None:
            keys, values = next_keys, values_of(follower[0], follower[3])

    loads[4].wait()
    out_ref[...] = (
        x_ref[...].astype(F32) + jnp.dot(att[...], wo[...], preferred_element_type=F32)
    ).astype(BF16)
    for copy in halo_copies + early_copies + late_copies:
        copy.wait_send()


def local(n_grp, n_rng, features, wq, wk, wv, wo, reach, peers, count, pick):
    rows, width = features.shape
    tiles = rows // TILE
    lanes = 2 * (width // HEADS)
    pairs = width // lanes
    early = list(range(1, n_grp - 2))
    late = list(range(n_grp - 2, n_grp))
    n_early, n_late = len(early) * PORTAL, len(late) * PORTAL
    smem = pl.BlockSpec(memory_space=pltpu.SMEM)
    hbm = pl.BlockSpec(memory_space=pltpu.HBM)

    def vmem(*shape, dtype=BF16):
        return pltpu.VMEM(shape, dtype)

    return pl.pallas_call(
        functools.partial(kernel, n_grp, n_rng, early, late),
        out_shape=jax.ShapeDtypeStruct((rows, width), BF16),
        in_specs=[hbm] * 5 + [smem] * 4,
        out_specs=pl.BlockSpec(memory_space=pltpu.VMEM),
        scratch_shapes=[
            vmem(rows, width),
            vmem(width, width),
            vmem(width, width),
            vmem(width, width),
            vmem(width, width),
            vmem(n_grp - 1, PORTAL, width),
            vmem(2, TILE, width),
            vmem(n_early, width),
            vmem(n_late, width),
            vmem(2, rows, width),
            vmem(rows, width),
            vmem(n_early, width),
            vmem(2 * TILE + n_late, width),
            vmem(pairs, 2, rows, lanes, dtype=F32),
            vmem(pairs, 2, rows, lanes, dtype=F32),
            vmem(rows, width),
            vmem(rows, rows, dtype=F32),
            vmem(2, TILE, TILE, dtype=F32),
            vmem(tiles, 1, n_early, dtype=F32),
            vmem(tiles, 1, n_late, dtype=F32),
            pltpu.SemaphoreType.DMA((5,)),
            pltpu.SemaphoreType.DMA((n_grp + 1,)),
            pltpu.SemaphoreType.DMA((n_grp + 1,)),
        ],
        compiler_params=pltpu.CompilerParams(collective_id=0, has_side_effects=True),
        name="graph_attention",
    )(features, wq, wk, wv, wo, reach, peers, count, pick)


def solution(mesh):
    return jax.shard_map(
        functools.partial(local, mesh.shape["grp"], mesh.shape["rng"]),
        mesh=mesh,
        in_specs=(
            P(("grp", "rng"), None),
            P(),
            P(),
            P(),
            P(),
            P(("grp", "rng")),
            P(("grp", "rng"), None),
            P(("grp", "rng")),
            P(("grp", "rng"), None),
        ),
        out_specs=P(("grp", "rng"), None),
        check_vma=False,
    )
```

profile of v0, /device:TPU:1, one launch (start us, length us, event | category | flops | bytes accessed | tf_op | source)
XLA Modules:
  0.0 28.7 jit_solution(12632294744167417588)
XLA Ops:
  0.7 26.1 %graph_attention.1 = bf16[256,1024]{1,0:T(8,128)(2,1)} custom-call(bf16[256,1024]{1,0:T(8,128)(2,1)} %feat_hbm.1, bf16[1024,1024]{1,0:T(8,128)(2,1)} %wq_hbm.1, bf16[1024,1024]{1,0:T(8,128)(2,1)} %wk_hbm.1, bf16[1024,1024]{1,0:T(8,128)(2,1)} %wv_hbm.1, bf16[1024,1024]{1,0:T(8,128)(2,1)} %wo_hbm.1, s32[1]{0:T(128)S(6)} %copy.11.reach_ref, s32[2,6]{1,0:T(2,128)} %peers_ref.1, ...), custom_call_target="tpu_custom_call" | custom-call | tf_op jit(solution)/shard_map/graph_attention/pallas_call | solution.py:335
  26.8 1.9 %copy.12 = bf16[256,1024]{1,0:T(8,128)(2,1)} copy(bf16[256,1024]{1,0:T(8,128)(2,1)} %graph_attention.1) | data formatting | bytes 1048576
where the time goes:
time: 28.9 us; the launch traced here: 28.7 us
  Pallas kernels  26.1 us (90%)
  local copies, waits for them, and re-layouts  1.87 us (6%)
  between operations  0.66 us (2%)
    pallas_call x1, Pallas kernels, local(): pl.pallas_call(functools.partial(kernel, n_grp, n_rng, early, late), out_...  26.1 us
    unnamed x1, local copies, waits for them, and re-layouts  1.87 us

commit v1 on v0

--- a/solution.py
+++ b/solution.py
@@ -12,6 +12,7 @@
 PORTAL = 64
 EPSILON = 1e-06
 LOG2E = 1.4426950408889634
+VMEM_LIMIT = 48 * 1024 * 1024
 MESH = pl.DeviceIdType.MESH
 F32 = jnp.float32
 BF16 = jnp.bfloat16
@@ -47,16 +48,20 @@
     wk_hbm,
     wv_hbm,
     wo_hbm,
+    reach_hbm,
+    peers_hbm,
+    count_hbm,
+    pick_hbm,
+    att,
+    x_ref,
+    wo,
+    wq,
+    wk,
+    wv,
     reach_ref,
     peers_ref,
     count_ref,
     pick_ref,
-    out_ref,
-    x_ref,
-    wq,
-    wk,
-    wv,
-    wo,
     stage,
     halo,
     port_e,
@@ -64,15 +69,16 @@
     q_s,
     xn_l,
     xn_e,
+    xn_h,
     xn_t,
     acc,
     top,
-    att,
     bias_l,
     bias_h,
     bias_e,
     bias_t,
     load_sem,
+    small_sem,
     send_sem,
     recv_sem,
 ):
@@ -89,7 +95,20 @@
             ((feat_hbm, x_ref), (wq_hbm, wq), (wk_hbm, wk), (wv_hbm, wv), (wo_hbm, wo))
         )
     ]
+    smalls = [
+        pltpu.make_async_copy(src, dst, small_sem.at[i])
+        for i, (src, dst) in enumerate(
+            (
+                (pick_hbm, pick_ref),
+                (reach_hbm, reach_ref),
+                (peers_hbm, peers_ref),
+                (count_hbm, count_ref),
+            )
+        )
+    ]
     loads[0].start()
+    for small in smalls:
+        small.start()
 
     above = lax.rem(rng + 1, n_rng)
     below = lax.rem(rng + n_rng - 1, n_rng)
@@ -101,9 +120,10 @@
             barrier, inc=1, device_id=(flipped(grp, offset), rng), device_id_type=MESH
         )
 
-    loads[0].wait()
     for load in loads[1:]:
         load.start()
+    smalls[0].wait()
+    loads[0].wait()
     for offset in range(1, n_grp):
         pick = jnp.full((PORTAL, width), pick_ref[0, flipped(grp, offset)], jnp.int32)
         chosen = x_ref[0:PORTAL, :]
@@ -124,11 +144,6 @@
         copy.start()
         return copy
 
-    halo_copies = [
-        remote(x_ref.at[pl.ds(rows - TILE, TILE)], halo.at[0], 0, (grp, above)),
-        remote(x_ref.at[pl.ds(0, TILE)], halo.at[1], 1, (grp, below)),
-    ]
-
     def send_portals(offsets, buffer):
         return [
             remote(
@@ -141,7 +156,13 @@
         ]
 
     early_copies = send_portals(early, port_e)
+    halo_copies = [
+        remote(x_ref.at[pl.ds(rows - TILE, TILE)], halo.at[0], 0, (grp, above)),
+        remote(x_ref.at[pl.ds(0, TILE)], halo.at[1], 1, (grp, below)),
+    ]
     late_copies = send_portals(late, port_t)
+    for small in smalls[1:]:
+        small.wait()
 
     reach = reach_ref[0]
     row_pos = lax.broadcasted_iota(jnp.int32, (rows, rows), 0)
@@ -227,34 +248,34 @@
             )
             top[pair, parity] = highest
 
-    def late_pair(pair, keys, values):
-        value_pair = split_values(values[2 * TILE :])
-        edges = []
+    def halo_pair(pair, keys, values):
         for side in range(2):
             span = slice(side * TILE, (side + 1) * TILE)
             place = slice(side * (rows - TILE), side * (rows - TILE) + TILE)
-            edges.append((nt_dot(q_pair(pair, place), keys[span]), split_values(values[span])))
-        both = nt_dot(q_pair(pair), keys[2 * TILE :])
+            both = nt_dot(q_pair(pair, place), keys[span])
+            value_pair = split_values(values[span])
+            for parity in range(2):
+                scores = both[parity * TILE : (parity + 1) * TILE] + bias_h[side]
+                before = top[pair, parity, place]
+                highest = jnp.maximum(before, jnp.max(scores, axis=1, keepdims=True))
+                weights = jnp.exp2(scores - widened(highest, scores.shape[1]))
+                acc[pair, parity, place] = acc[pair, parity, place] * jnp.exp2(
+                    before - highest
+                ) + product(weights, value_pair[parity])
+                top[pair, parity, place] = highest
+
+    def late_pair(pair, keys, values):
+        value_pair = split_values(values)
+        both = nt_dot(q_pair(pair), keys)
         halves = []
         for parity in range(2):
             scores = both[parity * rows : (parity + 1) * rows]
             scores = scores + spread(bias_t, scores.shape[1])
             before = top[pair, parity]
             highest = jnp.maximum(before, jnp.max(scores, axis=1, keepdims=True))
-            band = [
-                edge[parity * TILE : (parity + 1) * TILE] + bias_h[side]
-                for side, (edge, _) in enumerate(edges)
-            ]
-            sides = [jnp.max(part, axis=1, keepdims=True) for part in band]
-            low = jnp.maximum(highest[:TILE], sides[0])
-            high = jnp.maximum(highest[rows - TILE :], sides[1])
-            highest = stacked(low, highest[TILE : rows - TILE], high)
+            weights = jnp.exp2(scores - widened(highest, scores.shape[1]))
             mixed = acc[pair, parity] * jnp.exp2(before - highest)
-            weights = jnp.exp2(scores - widened(highest, scores.shape[1]))
-            mixed = mixed + product(weights, value_pair[parity])
-            low = mixed[:TILE] + product(jnp.exp2(band[0] - low), edges[0][1][parity])
-            high = mixed[rows - TILE :] + product(jnp.exp2(band[1] - high), edges[1][1][parity])
-            halves.append(stacked(low, mixed[TILE : rows - TILE], high))
+            halves.append(mixed + product(weights, value_pair[parity]))
         left = lax.broadcasted_iota(jnp.int32, (rows, lanes), 1) < head_dim
         even, odd = halves
         total = pltpu.roll(jnp.where(left, odd, even), head_dim, 1)
@@ -283,16 +304,21 @@
             copy.wait_recv()
         xn_e[...] = rms_normed(port_e[...])
 
+    def halo_ready():
+        for copy in halo_copies:
+            copy.wait_recv()
+        xn_h[...] = rms_normed(halo[...].reshape(2 * TILE, width))
+
     def late_ready():
-        for copy in halo_copies + late_copies:
+        for copy in late_copies:
             copy.wait_recv()
-        xn_t[: 2 * TILE] = rms_normed(halo[...].reshape(2 * TILE, width))
-        xn_t[2 * TILE :] = rms_normed(port_t[...])
+        xn_t[...] = rms_normed(port_t[...])
 
     steps = []
     for source, ready, attend in (
         (xn_l, None, local_pair),
         (xn_e, early_ready, early_pair),
+        (xn_h, halo_ready, halo_pair),
         (xn_t, late_ready, late_pair),
     ):
         for part in range(width // block):
@@ -311,11 +337,23 @@
             keys, values = next_keys, values_of(follower[0], follower[3])
 
     loads[4].wait()
-    out_ref[...] = (
-        x_ref[...].astype(F32) + jnp.dot(att[...], wo[...], preferred_element_type=F32)
-    ).astype(BF16)
     for copy in halo_copies + early_copies + late_copies:
         copy.wait_send()
+
+
+def project_kernel(att_ref, x_ref, wo_ref, out_hbm, out_v, sem):
+    width = out_v.shape[1]
+    block = width // 4
+    copies = []
+    for part in range(4):
+        cols = slice(part * block, (part + 1) * block)
+        mixed = jnp.dot(att_ref[...], wo_ref[:, cols], preferred_element_type=F32)
+        out_v[:, cols] = (x_ref[:, cols].astype(F32) + mixed).astype(BF16)
+        copy = pltpu.make_async_copy(out_v.at[:, cols], out_hbm.at[:, cols], sem.at[part])
+        copy.start()
+        copies.append(copy)
+    for copy in copies:
+        copy.wait()
 
 
 def local(n_grp, n_rng, features, wq, wk, wv, wo, reach, peers, count, pick):
@@ -326,23 +364,28 @@
     early = list(range(1, n_grp - 2))
     late = list(range(n_grp - 2, n_grp))
     n_early, n_late = len(early) * PORTAL, len(late) * PORTAL
-    smem = pl.BlockSpec(memory_space=pltpu.SMEM)
     hbm = pl.BlockSpec(memory_space=pltpu.HBM)
+    whole = pl.BlockSpec(memory_space=pltpu.VMEM)
 
     def vmem(*shape, dtype=BF16):
         return pltpu.VMEM(shape, dtype)
 
-    return pl.pallas_call(
+    def held(array):
+        return pltpu.with_memory_space_constraint(array, pltpu.HBM)
+
+    att, x, wo = pl.pallas_call(
         functools.partial(kernel, n_grp, n_rng, early, late),
-        out_shape=jax.ShapeDtypeStruct((rows, width), BF16),
-        in_specs=[hbm] * 5 + [smem] * 4,
-        out_specs=pl.BlockSpec(memory_space=pltpu.VMEM),
+        out_shape=(vmem(rows, width), vmem(rows, width), vmem(width, width)),
+        in_specs=[hbm] * 9,
+        out_specs=(whole,) * 3,
         scratch_shapes=[
-            vmem(rows, width),
             vmem(width, width),
             vmem(width, width),
             vmem(width, width),
-            vmem(width, width),
+            pltpu.SMEM(reach.shape, jnp.int32),
+            pltpu.SMEM(peers.shape, jnp.int32),
+            pltpu.SMEM(count.shape, jnp.int32),
+            pltpu.SMEM(pick.shape, jnp.int32),
             vmem(n_grp - 1, PORTAL, width),
             vmem(2, TILE, width),
             vmem(n_early, width),
@@ -350,21 +393,33 @@
             vmem(2, rows, width),
             vmem(rows, width),
             vmem(n_early, width),
-            vmem(2 * TILE + n_late, width),
+            vmem(2 * TILE, width),
+            vmem(n_late, width),
             vmem(pairs, 2, rows, lanes, dtype=F32),
             vmem(pairs, 2, rows, lanes, dtype=F32),
-            vmem(rows, width),
             vmem(rows, rows, dtype=F32),
             vmem(2, TILE, TILE, dtype=F32),
             vmem(tiles, 1, n_early, dtype=F32),
             vmem(tiles, 1, n_late, dtype=F32),
             pltpu.SemaphoreType.DMA((5,)),
+            pltpu.SemaphoreType.DMA((4,)),
             pltpu.SemaphoreType.DMA((n_grp + 1,)),
             pltpu.SemaphoreType.DMA((n_grp + 1,)),
         ],
-        compiler_params=pltpu.CompilerParams(collective_id=0, has_side_effects=True),
+        compiler_params=pltpu.CompilerParams(
+            collective_id=0, has_side_effects=True, vmem_limit_bytes=VMEM_LIMIT
+        ),
         name="graph_attention",
-    )(features, wq, wk, wv, wo, reach, peers, count, pick)
+    )(*map(held, (features, wq, wk, wv, wo)), reach, *map(held, (peers, count, pick)))
+    return pl.pallas_call(
+        project_kernel,
+        out_shape=jax.ShapeDtypeStruct((rows, width), BF16),
+        in_specs=[whole] * 3,
+        out_specs=hbm,
+        scratch_shapes=[vmem(rows, width), pltpu.SemaphoreType.DMA((4,))],
+        compiler_params=pltpu.CompilerParams(vmem_limit_bytes=VMEM_LIMIT // 4),
+        name="out_projection",
+    )(att, x, wo)
 
 
 def solution(mesh):

time: 28.9 us -> 27.5 us (0.952)
  the two profiles are of different devices: /device:TPU:1 before, /device:TPU:0 now
where the time goes in v1:
time: 27.5 us; the launch traced here: 27.3 us
  Pallas kernels  26.6 us (97%)
  between operations  0.66 us (2%)
    pallas_call x1, Pallas kernels, local(): pl.pallas_call(functools.partial(kernel, n_grp, n_rng, early, late), out_...  25.2 us
    pallas_call x1, Pallas kernels, local(): pl.pallas_call(project_kernel, out_shape=jax.ShapeDtypeStruct((rows, widt...  1.46 us

profile of v1, /device:TPU:0, one launch (start us, length us, event | category | flops | bytes accessed | tf_op | source)
XLA Modules:
  0.0 27.3 jit_solution(5765195209947100036)
XLA Ops:
  0.7 25.2 %graph_attention.1 = (bf16[256,1024]{1,0:T(8,128)(2,1)S(1)}, bf16[256,1024]{1,0:T(8,128)(2,1)S(1)}, bf16[1024,1024]{1,0:T(8,128)(2,1)S(1)}) custom-call(bf16[256,1024]{1,0:T(8,128)(2,1)} %feat_hbm.1, bf16[1024,1024]{1,0:T(8,128)(2,1)} %wq_hbm.1, bf16[1024,1024]{1,0:T(8,128)(2,1)} %wk_hbm.1, bf16[1024,1024]{1,0:T(8,128)(2,1)} %wv_hbm.1, ...), custom_call_target="tpu_custom_call" | custom-call | tf_op jit(solution)/shard_map/graph_attention/pallas_call | solution.py:376
  25.8 1.5 %out_projection.1 = bf16[256,1024]{1,0:T(8,128)(2,1)} custom-call(bf16[256,1024]{1,0:T(8,128)(2,1)S(1)} %get-tuple-element.8.att_ref, bf16[256,1024]{1,0:T(8,128)(2,1)S(1)} %get-tuple-element.9.x_ref, bf16[1024,1024]{1,0:T(8,128)(2,1)S(1)} %get-tuple-element.10.wo_ref), custom_call_target="tpu_custom_call" | custom-call | tf_op jit(solution)/shard_map/out_projection/pallas_call | solution.py:414

commit v2 on v1

v2 whole, which is shorter than its diff:
```python
import functools

import jax
import jax.numpy as jnp
from jax import lax
from jax.experimental import pallas as pl
from jax.experimental.pallas import tpu as pltpu
from jax.sharding import PartitionSpec as P

HEADS = 16
TILE = 128
PORTAL = 64
QUAD = 4
EPSILON = 1e-06
LOG2E = 1.4426950408889634
VMEM_LIMIT = 48 * 1024 * 1024
MESH = pl.DeviceIdType.MESH
F32 = jnp.float32
BF16 = jnp.bfloat16


def flipped(index, offset):
    result = index
    bit = 1
    while bit <= offset:
        if offset & bit:
            result = result + bit * (1 - 2 * ((index // bit) % 2))
        bit *= 2
    return result


def rms_normed(rows):
    widened = rows.astype(F32)
    factor = lax.rsqrt(jnp.mean(widened * widened, axis=1, keepdims=True) + EPSILON)
    return (widened * factor).astype(BF16)


def stage_plan(n_grp, rows):
    half, near = PORTAL // 2, TILE // 2
    far = near // 2
    late = (n_grp - 2, n_grp - 1)
    early = range(1, n_grp - 2)

    def portals(offsets, first, size):
        return [("portal", offset, first, size) for offset in offsets]

    def halo(distance, size):
        return [
            ("below", None, rows - distance - size, size),
            ("above", None, distance, size),
        ]

    return [
        portals([o for o in early if o == 1 or o % 2 == 0], 0, PORTAL),
        portals([o for o in early if o != 1 and o % 2 == 1], 0, PORTAL),
        halo(0, near),
        portals(late, 0, half) + halo(near, far),
        portals(late, half, half) + halo(near + far, far),
    ]


def stage_rows(blocks):
    return sum(block[3] for block in blocks)


def kernel(n_grp, n_rng, plan, *refs):
    feat_hbm, wq_hbm, wk_hbm, wv_hbm, wo_hbm, reach_hbm, peers_hbm, count_hbm, pick_hbm = refs[:9]
    att, x_ref, wo = refs[9:12]
    wq, wk, wv, reach_ref, peers_ref, count_ref, pick_ref, stage = refs[12:20]
    landed = refs[20 : 20 + len(plan)]
    biases = refs[20 + len(plan) : 21 + 2 * len(plan)]
    xn, q_t, acc, top, total, load_sem, small_sem, send_sem, recv_sem = refs[21 + 2 * len(plan) :]
    rows, width = x_ref.shape
    tiles = rows // TILE
    head_dim = width // HEADS
    block = QUAD * head_dim
    grp = lax.axis_index("grp")
    rng = lax.axis_index("rng")
    loads = [
        pltpu.make_async_copy(src, dst, load_sem.at[i])
        for i, (src, dst) in enumerate(
            ((feat_hbm, x_ref), (wq_hbm, wq), (wk_hbm, wk), (wv_hbm, wv), (wo_hbm, wo))
        )
    ]
    smalls = [
        pltpu.make_async_copy(src, dst, small_sem.at[i])
        for i, (src, dst) in enumerate(
            (
                (pick_hbm, pick_ref),
                (reach_hbm, reach_ref),
                (peers_hbm, peers_ref),
                (count_hbm, count_ref),
            )
        )
    ]
    loads[0].start()
    for small in smalls:
        small.start()

    above = lax.rem(rng + 1, n_rng)
    below = lax.rem(rng + n_rng - 1, n_rng)
    barrier = pltpu.get_barrier_semaphore()
    for other in (above, below):
        pl.semaphore_signal(barrier, inc=1, device_id=(grp, other), device_id_type=MESH)
    for offset in range(1, n_grp):
        pl.semaphore_signal(
            barrier, inc=1, device_id=(flipped(grp, offset), rng), device_id_type=MESH
        )

    for load in loads[1:]:
        load.start()
    smalls[0].wait()
    loads[0].wait()
    for offset in range(1, n_grp):
        pick = jnp.full((PORTAL, width), pick_ref[0, flipped(grp, offset)], jnp.int32)
        chosen = x_ref[0:PORTAL, :]
        for i in range(1, rows // PORTAL):
            chosen = jnp.where(pick == i, x_ref[i * PORTAL : (i + 1) * PORTAL, :], chosen)
        stage[offset - 1] = chosen
    pl.semaphore_wait(barrier, n_grp + 1)

    arrivals = []
    slot = 0
    for blocks, buffer in zip(plan, landed):
        copies = []
        place = 0
        for kind, offset, first, size in blocks:
            if kind == "portal":
                src = stage.at[offset - 1, pl.ds(first, size)]
                device = (flipped(grp, offset), rng)
            else:
                src = x_ref.at[pl.ds(first, size)]
                device = (grp, above if kind == "below" else below)
            copy = pltpu.make_async_remote_copy(
                src_ref=src,
                dst_ref=buffer.at[pl.ds(place, size)],
                send_sem=send_sem.at[slot],
                recv_sem=recv_sem.at[slot],
                device_id=device,
                device_id_type=MESH,
            )
            copy.start()
            copies.append(copy)
            place += size
            slot += 1
        arrivals.append(copies)
    for small in smalls[1:]:
        small.wait()

    reach = reach_ref[0]
    places = lax.broadcasted_iota(jnp.int32, (rows, rows), 1)
    steps = lax.broadcasted_iota(jnp.int32, (rows, rows), 0)
    biases[0][...] = jnp.where(jnp.abs(places - steps) <= reach, 0.0, -jnp.inf)
    for blocks, bias in zip(plan, biases[1:]):
        place = 0
        for kind, offset, first, size in blocks:
            span = slice(place, place + size)
            if kind == "portal":
                source = flipped(grp, offset)
                tile = lax.broadcasted_iota(jnp.int32, (size, rows), 1) // TILE
                live = jnp.zeros((size, rows), jnp.int32)
                for t in range(tiles):
                    listed = jnp.int32(0)
                    for s in range(peers_ref.shape[1]):
                        used = jnp.logical_and(s < count_ref[t], peers_ref[t, s] == source)
                        listed = listed + used.astype(jnp.int32)
                    live = jnp.where(tile == t, listed, live)
                bias[span] = jnp.where(live > 0, 0.0, -jnp.inf)
            else:
                base = first - rows if kind == "below" else first + rows
                gap = steps[:size] + base - places[:size]
                bias[span] = jnp.where(jnp.abs(gap) <= reach, 0.0, -jnp.inf)
            place += size

    scale = head_dim ** (-0.5) * LOG2E

    def projected(source, weight, part):
        return jnp.dot(
            source, weight[:, part * block : (part + 1) * block], preferred_element_type=F32
        )

    def head_only(keys, head):
        column = lax.broadcasted_iota(jnp.int32, keys.shape, 1)
        return jnp.where(column // head_dim == head, keys, jnp.zeros_like(keys))

    def scores_of(part, keys):
        count = keys.shape[0]
        lhs = jnp.concatenate([head_only(keys, head) for head in range(QUAD)], axis=0)
        queries = q_t[part * block : (part + 1) * block, :]
        stacked = jnp.dot(lhs, queries, preferred_element_type=F32)
        return [stacked[head * count : (head + 1) * count] for head in range(QUAD)]

    def weights_of(part, raw, bias, first, last):
        found = []
        for head in range(QUAD):
            number = part * QUAD + head
            scores = raw[head] + bias[...]
            highest = jnp.max(scores, axis=0, keepdims=True)
            shrink = None
            if not first:
                before = top[number : number + 1, :]
                highest = jnp.maximum(highest, before)
                shrink = jnp.exp2(before - highest)
            weights = jnp.exp2(scores - highest)
            sums = jnp.sum(weights.reshape(weights.shape[0] // 8, 8, rows), axis=0)
            if not last:
                top[number : number + 1, :] = highest
            found.append((weights.astype(BF16), sums, shrink))
        return found

    def mix(part, values, found, first, last):
        done = []
        for head in range(QUAD):
            number = part * QUAD + head
            span = slice(number * head_dim, (number + 1) * head_dim)
            weights, sums, shrink = found[head]
            mixed = jnp.dot(
                values[head * head_dim : (head + 1) * head_dim],
                weights,
                preferred_element_type=F32,
            )
            if not first:
                sums = sums + total[number] * shrink
                mixed = mixed + acc[span] * shrink
            if last:
                whole = jnp.sum(sums, axis=0, keepdims=True)
                done.append((mixed * (1.0 / whole)).astype(BF16))
            else:
                total[number] = sums
                acc[span] = mixed
        if last:
            att[:, part * block : (part + 1) * block] = jnp.concatenate(done, axis=0).T

    def run_stage(source, bias, first, last):
        parts = width // block
        keys = [projected(source[...], wk, part).astype(BF16) for part in range(parts)]

        def values_of(part):
            return projected(source[...], wv, part).astype(BF16).T

        if source.shape[0] <= TILE:
            raw = [scores_of(part, keys[part]) for part in range(parts)]
            values = [values_of(part) for part in range(parts)]
            for part in range(parts):
                found = weights_of(part, raw[part], bias, first, last)
                mix(part, values[part], found, first, last)
            return
        waiting = None
        for part in range(parts):
            raw = scores_of(part, keys[part])
            values = values_of(part)
            found = weights_of(part, raw, bias, first, last)
            if waiting is not None:
                mix(*waiting, first, last)
            waiting = (part, values, found)
        mix(*waiting, first, last)

    xn[0:rows] = rms_normed(x_ref[...])
    loads[1].wait()
    for part in range(width // block):
        queries = (projected(xn[0:rows], wq, part) * scale).astype(BF16)
        q_t[part * block : (part + 1) * block, :] = queries.T
    loads[2].wait()
    loads[3].wait()
    run_stage(xn.at[pl.ds(0, rows)], biases[0], True, False)
    place = rows
    for number, (copies, buffer) in enumerate(zip(arrivals, landed)):
        for copy in copies:
            copy.wait_recv()
        size = buffer.shape[0]
        xn[place : place + size] = rms_normed(buffer[...])
        run_stage(
            xn.at[pl.ds(place, size)], biases[number + 1], False, number + 1 == len(plan)
        )
        place += size

    loads[4].wait()
    for copies in arrivals:
        for copy in copies:
            copy.wait_send()


def project_kernel(att_ref, x_ref, wo_ref, out_hbm, out_v, sem):
    width = out_v.shape[1]
    block = width // 4
    copies = []
    for part in range(4):
        cols = slice(part * block, (part + 1) * block)
        mixed = jnp.dot(att_ref[...], wo_ref[:, cols], preferred_element_type=F32)
        out_v[:, cols] = (x_ref[:, cols].astype(F32) + mixed).astype(BF16)
        copy = pltpu.make_async_copy(out_v.at[:, cols], out_hbm.at[:, cols], sem.at[part])
        copy.start()
        copies.append(copy)
    for copy in copies:
        copy.wait()


def local(n_grp, n_rng, features, wq, wk, wv, wo, reach, peers, count, pick):
    rows, width = features.shape
    plan = stage_plan(n_grp, rows)
    sizes = [stage_rows(blocks) for blocks in plan]
    n_copies = sum(len(blocks) for blocks in plan)
    hbm = pl.BlockSpec(memory_space=pltpu.HBM)
    whole = pl.BlockSpec(memory_space=pltpu.VMEM)

    def vmem(*shape, dtype=BF16):
        return pltpu.VMEM(shape, dtype)

    def held(array):
        return pltpu.with_memory_space_constraint(array, pltpu.HBM)

    att, x, wo = pl.pallas_call(
        functools.partial(kernel, n_grp, n_rng, plan),
        out_shape=(vmem(rows, width), vmem(rows, width), vmem(width, width)),
        in_specs=[hbm] * 9,
        out_specs=(whole,) * 3,
        scratch_shapes=[
            vmem(width, width),
            vmem(width, width),
            vmem(width, width),
            pltpu.SMEM(reach.shape, jnp.int32),
            pltpu.SMEM(peers.shape, jnp.int32),
            pltpu.SMEM(count.shape, jnp.int32),
            pltpu.SMEM(pick.shape, jnp.int32),
            vmem(n_grp - 1, PORTAL, width),
            *(vmem(size, width) for size in sizes),
            *(vmem(size, rows, dtype=F32) for size in [rows] + sizes),
            vmem(rows + sum(sizes), width),
            vmem(width, rows),
            vmem(width, rows, dtype=F32),
            vmem(HEADS, rows, dtype=F32),
            vmem(HEADS, 8, rows, dtype=F32),
            pltpu.SemaphoreType.DMA((5,)),
            pltpu.SemaphoreType.DMA((4,)),
            pltpu.SemaphoreType.DMA((n_copies,)),
            pltpu.SemaphoreType.DMA((n_copies,)),
        ],
        compiler_params=pltpu.CompilerParams(
            collective_id=0, has_side_effects=True, vmem_limit_bytes=VMEM_LIMIT
        ),
        name="graph_attention",
    )(*map(held, (features, wq, wk, wv, wo)), reach, *map(held, (peers, count, pick)))
    return pl.pallas_call(
        project_kernel,
        out_shape=jax.ShapeDtypeStruct((rows, width), BF16),
        in_specs=[whole] * 3,
        out_specs=hbm,
        scratch_shapes=[vmem(rows, width), pltpu.SemaphoreType.DMA((4,))],
        compiler_params=pltpu.CompilerParams(vmem_limit_bytes=VMEM_LIMIT // 4),
        name="out_projection",
    )(att, x, wo)


def solution(mesh):
    return jax.shard_map(
        functools.partial(local, mesh.shape["grp"], mesh.shape["rng"]),
        mesh=mesh,
        in_specs=(
            P(("grp", "rng"), None),
            P(),
            P(),
            P(),
            P(),
            P(("grp", "rng")),
            P(("grp", "rng"), None),
            P(("grp", "rng")),
            P(("grp", "rng"), None),
        ),
        out_specs=P(("grp", "rng"), None),
        check_vma=False,
    )
```

time: 27.5 us -> 23.3 us (0.85)
  Pallas kernels: 26.6 us -> 22.5 us
    pallas_call x1, Pallas kernels: 25.2 us -> 21 us  [local(): pl.pallas_call(functools.partial(kernel, n_grp, n_rng, plan), out_shape=(...]
where the time goes in v2:
time: 23.3 us; the launch traced here: 23.1 us
  Pallas kernels  22.5 us (97%)
  between operations  0.66 us (3%)
    pallas_call x1, Pallas kernels, local(): pl.pallas_call(functools.partial(kernel, n_grp, n_rng, plan), out_shape=(...  21 us
    pallas_call x1, Pallas kernels, local(): pl.pallas_call(project_kernel, out_shape=jax.ShapeDtypeStruct((rows, widt...  1.46 us

profile of v2, /device:TPU:0, one launch (start us, length us, event | category | flops | bytes accessed | tf_op | source)
XLA Modules:
  0.0 23.1 jit_solution(18433170454254350286)
XLA Ops:
  0.7 21.0 %graph_attention.1 = (bf16[256,1024]{1,0:T(8,128)(2,1)S(1)}, bf16[256,1024]{1,0:T(8,128)(2,1)S(1)}, bf16[1024,1024]{1,0:T(8,128)(2,1)S(1)}) custom-call(bf16[256,1024]{1,0:T(8,128)(2,1)} %refs_0_.1, bf16[1024,1024]{1,0:T(8,128)(2,1)} %refs_1_.1, bf16[1024,1024]{1,0:T(8,128)(2,1)} %refs_2_.1, bf16[1024,1024]{1,0:T(8,128)(2,1)} %refs_3_.1, ...), custom_call_target="tpu_custom_call" | custom-call | tf_op jit(solution)/shard_map/graph_attention/pallas_call | solution.py:312
  21.7 1.5 %out_projection.1 = bf16[256,1024]{1,0:T(8,128)(2,1)} custom-call(bf16[256,1024]{1,0:T(8,128)(2,1)S(1)} %get-tuple-element.8.att_ref, bf16[256,1024]{1,0:T(8,128)(2,1)S(1)} %get-tuple-element.9.x_ref, bf16[1024,1024]{1,0:T(8,128)(2,1)S(1)} %get-tuple-element.10.wo_ref), custom_call_target="tpu_custom_call" | custom-call | tf_op jit(solution)/shard_map/out_projection/pallas_call | solution.py:343

commit v3 on v2

--- a/solution.py
+++ b/solution.py
@@ -50,11 +50,12 @@
             ("above", None, distance, size),
         ]
 
+    odd = [o for o in early if o > 1 and o % 2 == 1]
     return [
-        portals([o for o in early if o == 1 or o % 2 == 0], 0, PORTAL),
-        portals([o for o in early if o != 1 and o % 2 == 1], 0, PORTAL),
-        halo(0, near),
-        portals(late, 0, half) + halo(near, far),
+        portals([o for o in early if o not in odd], 0, PORTAL),
+        portals(odd[:-1], 0, PORTAL) + halo(0, near)[:1],
+        halo(0, near)[1:] + portals(late, 0, half),
+        portals(odd[-1:], 0, PORTAL) + halo(near, far),
         portals(late, half, half) + halo(near + far, far),
     ]
 
@@ -69,7 +70,7 @@
     wq, wk, wv, reach_ref, peers_ref, count_ref, pick_ref, stage = refs[12:20]
     landed = refs[20 : 20 + len(plan)]
     biases = refs[20 + len(plan) : 21 + 2 * len(plan)]
-    xn, q_t, acc, top, total, load_sem, small_sem, send_sem, recv_sem = refs[21 + 2 * len(plan) :]
+    xn, q_t, acc, top, total, load_sem, small_sem, send_sem, recv_sem, answer = refs[21 + 2 * len(plan) :]
     rows, width = x_ref.shape
     tiles = rows // TILE
     head_dim = width // HEADS
@@ -99,16 +100,67 @@
 
     above = lax.rem(rng + 1, n_rng)
     below = lax.rem(rng + n_rng - 1, n_rng)
+    chip = grp // 2
+
+    def crossed(offset):
+        bits = [bit for bit in range(n_grp.bit_length()) if (offset // 2) >> bit & 1]
+        held = sum((chip // (1 << bit)) % 2 for bit in bits)
+        return jnp.logical_and(held > 0, held < len(bits))
+
+    peers = []
+    for offset in range(1, n_grp):
+        other = flipped(grp, offset)
+        apart = crossed(offset)
+        straight = jnp.logical_not(apart)
+        greets = jnp.logical_and(straight, grp < other)
+        answers = jnp.logical_and(straight, grp > other)
+        peers.append(((other, rng), greets, answers, jnp.logical_or(greets, apart), offset - 1))
+    peers.append(((grp, above), rng < above, rng > above, rng < above, n_grp))
+    peers.append(((grp, below), rng < below, rng > below, rng < below, n_grp - 1))
     barrier = pltpu.get_barrier_semaphore()
-    for other in (above, below):
-        pl.semaphore_signal(barrier, inc=1, device_id=(grp, other), device_id_type=MESH)
-    for offset in range(1, n_grp):
-        pl.semaphore_signal(
-            barrier, inc=1, device_id=(flipped(grp, offset), rng), device_id_type=MESH
-        )
+    greeted = jnp.int32(0)
+    for device, greets, answers, _, _ in peers:
+
+        @pl.when(greets)
+        def _greet(device=device):
+            pl.semaphore_signal(barrier, inc=1, device_id=device, device_id_type=MESH)
+
+        greeted = greeted + answers.astype(jnp.int32)
+
+    def tell(number, device):
+        pl.semaphore_signal(answer.at[number], inc=1, device_id=device, device_id_type=MESH)
+
+    def ready(number):
+        @pl.when(peers[number][3])
+        def _wait():
+            pl.semaphore_wait(answer.at[number], 1)
+
+    def introduce():
+        for first in range(2, n_grp, 2):
+            for second in range(first + 2, n_grp):
+                if (first // 2) & (second // 2):
+                    continue
+                bits = [bit for bit in range(n_grp.bit_length()) if ((first | second) // 2) >> bit & 1]
+                held = sum((chip // (1 << bit)) % 2 for bit in bits)
+
+                @pl.when(held == 0)
+                def _introduce(first=first, second=second):
+                    tell((first ^ second) - 1, (flipped(grp, first), rng))
+                    tell((first ^ second) - 1, (flipped(grp, second), rng))
 
     for load in loads[1:]:
         load.start()
+
+    @pl.when(greeted > 0)
+    def _greeted():
+        pl.semaphore_wait(barrier, greeted)
+
+    for device, _, answers, _, theirs in peers:
+
+        @pl.when(answers)
+        def _answer(device=device, theirs=theirs):
+            tell(theirs, device)
+
     smalls[0].wait()
     loads[0].wait()
     for offset in range(1, n_grp):
@@ -117,33 +169,61 @@
         for i in range(1, rows // PORTAL):
             chosen = jnp.where(pick == i, x_ref[i * PORTAL : (i + 1) * PORTAL, :], chosen)
         stage[offset - 1] = chosen
-    pl.semaphore_wait(barrier, n_grp + 1)
-
-    arrivals = []
-    slot = 0
-    for blocks, buffer in zip(plan, landed):
-        copies = []
-        place = 0
-        for kind, offset, first, size in blocks:
-            if kind == "portal":
-                src = stage.at[offset - 1, pl.ds(first, size)]
-                device = (flipped(grp, offset), rng)
-            else:
-                src = x_ref.at[pl.ds(first, size)]
-                device = (grp, above if kind == "below" else below)
-            copy = pltpu.make_async_remote_copy(
-                src_ref=src,
-                dst_ref=buffer.at[pl.ds(place, size)],
-                send_sem=send_sem.at[slot],
-                recv_sem=recv_sem.at[slot],
-                device_id=device,
-                device_id_type=MESH,
-            )
-            copy.start()
-            copies.append(copy)
-            place += size
-            slot += 1
-        arrivals.append(copies)
+
+    def send(kinds):
+        for number, (blocks, buffer) in enumerate(zip(plan, landed)):
+            place = 0
+            for kind, offset, first, size in blocks:
+                if kind == "portal":
+                    src = stage.at[offset - 1, pl.ds(first, size)]
+                    device = (flipped(grp, offset), rng)
+                else:
+                    src = x_ref.at[pl.ds(first, size)]
+                    device = (grp, above if kind == "below" else below)
+                if (kind, offset) in kinds:
+                    pltpu.make_async_remote_copy(
+                        src_ref=src,
+                        dst_ref=buffer.at[pl.ds(place, size)],
+                        send_sem=send_sem.at[0],
+                        recv_sem=recv_sem.at[number],
+                        device_id=device,
+                        device_id_type=MESH,
+                    ).start()
+                place += size
+
+    def arrived(number):
+        buffer = landed[number]
+        pltpu.make_async_remote_copy(
+            src_ref=buffer,
+            dst_ref=buffer,
+            send_sem=send_sem.at[0],
+            recv_sem=recv_sem.at[number],
+            device_id=(grp, above),
+            device_id_type=MESH,
+        ).wait_recv()
+
+    direct = list(range(1, n_grp - 2))
+    for offset in [o for o in direct if o % 2 == 0] + [o for o in direct if o % 2 == 1]:
+        ready(offset - 1)
+        send([("portal", offset)])
+    introduce()
+    ready(n_grp - 1)
+
+    @pl.when(jnp.logical_and(rng > 0, rng < n_rng - 1))
+    def _send_both():
+        ready(n_grp)
+        send([("below", None), ("above", None)])
+
+    @pl.when(rng == n_rng - 1)
+    def _send_round_first():
+        ready(n_grp)
+        send([("below", None)])
+        send([("above", None)])
+
+    @pl.when(rng == 0)
+    def _send_up():
+        send([("below", None)])
+
     for small in smalls[1:]:
         small.wait()
 
@@ -260,13 +340,21 @@
     for part in range(width // block):
         queries = (projected(xn[0:rows], wq, part) * scale).astype(BF16)
         q_t[part * block : (part + 1) * block, :] = queries.T
+    for offset in range(n_grp - 2, n_grp):
+        ready(offset - 1)
+    send([("portal", offset) for offset in range(n_grp - 2, n_grp)])
+
+    @pl.when(rng == 0)
+    def _send_round():
+        ready(n_grp)
+        send([("above", None)])
+
     loads[2].wait()
     loads[3].wait()
     run_stage(xn.at[pl.ds(0, rows)], biases[0], True, False)
     place = rows
-    for number, (copies, buffer) in enumerate(zip(arrivals, landed)):
-        for copy in copies:
-            copy.wait_recv()
+    for number, buffer in enumerate(landed):
+        arrived(number)
         size = buffer.shape[0]
         xn[place : place + size] = rms_normed(buffer[...])
         run_stage(
@@ -275,9 +363,15 @@
         place += size
 
     loads[4].wait()
-    for copies in arrivals:
-        for copy in copies:
-            copy.wait_send()
+    sent = xn.at[pl.ds(rows, place - rows)]
+    pltpu.make_async_remote_copy(
+        src_ref=sent,
+        dst_ref=sent,
+        send_sem=send_sem.at[0],
+        recv_sem=recv_sem.at[0],
+        device_id=(grp, above),
+        device_id_type=MESH,
+    ).wait_send()
 
 
 def project_kernel(att_ref, x_ref, wo_ref, out_hbm, out_v, sem):
@@ -299,7 +393,6 @@
     rows, width = features.shape
     plan = stage_plan(n_grp, rows)
     sizes = [stage_rows(blocks) for blocks in plan]
-    n_copies = sum(len(blocks) for blocks in plan)
     hbm = pl.BlockSpec(memory_space=pltpu.HBM)
     whole = pl.BlockSpec(memory_space=pltpu.VMEM)
 
@@ -332,8 +425,9 @@
             vmem(HEADS, 8, rows, dtype=F32),
             pltpu.SemaphoreType.DMA((5,)),
             pltpu.SemaphoreType.DMA((4,)),
-            pltpu.SemaphoreType.DMA((n_copies,)),
-            pltpu.SemaphoreType.DMA((n_copies,)),
+            pltpu.SemaphoreType.DMA((1,)),
+            pltpu.SemaphoreType.DMA((len(plan),)),
+            pltpu.SemaphoreType.REGULAR((n_grp + 1,)),
         ],
         compiler_params=pltpu.CompilerParams(
             collective_id=0, has_side_effects=True, vmem_limit_bytes=VMEM_LIMIT

time: 23.3 us -> 22.4 us (0.961)
  Pallas kernels: 22.5 us -> 21.5 us
    pallas_call x1, Pallas kernels: 21 us -> 20.1 us  [local(): pl.pallas_call(functools.partial(kernel, n_grp, n_rng, plan), out_shape=(...]
where the time goes in v3:
time: 22.4 us; the launch traced here: 22.2 us
  Pallas kernels  21.5 us (96%)
  between operations  0.66 us (3%)
    pallas_call x1, Pallas kernels, local(): pl.pallas_call(functools.partial(kernel, n_grp, n_rng, plan), out_shape=(...  20.1 us
    pallas_call x1, Pallas kernels, local(): pl.pallas_call(project_kernel, out_shape=jax.ShapeDtypeStruct((rows, widt...  1.46 us

profile of v3, /device:TPU:0, one launch (start us, length us, event | category | flops | bytes accessed | tf_op | source)
XLA Modules:
  0.0 22.2 jit_solution(753262424532100186)
XLA Ops:
  0.7 20.1 %graph_attention.1 = (bf16[256,1024]{1,0:T(8,128)(2,1)S(1)}, bf16[256,1024]{1,0:T(8,128)(2,1)S(1)}, bf16[1024,1024]{1,0:T(8,128)(2,1)S(1)}) custom-call(bf16[256,1024]{1,0:T(8,128)(2,1)} %refs_0_.1, bf16[1024,1024]{1,0:T(8,128)(2,1)} %refs_1_.1, bf16[1024,1024]{1,0:T(8,128)(2,1)} %refs_2_.1, bf16[1024,1024]{1,0:T(8,128)(2,1)} %refs_3_.1, ...), custom_call_target="tpu_custom_call" | custom-call | tf_op jit(solution)/shard_map/graph_attention/pallas_call | solution.py:405
  20.7 1.5 %out_projection.1 = bf16[256,1024]{1,0:T(8,128)(2,1)} custom-call(bf16[256,1024]{1,0:T(8,128)(2,1)S(1)} %get-tuple-element.8.att_ref, bf16[256,1024]{1,0:T(8,128)(2,1)S(1)} %get-tuple-element.9.x_ref, bf16[1024,1024]{1,0:T(8,128)(2,1)S(1)} %get-tuple-element.10.wo_ref), custom_call_target="tpu_custom_call" | custom-call | tf_op jit(solution)/shard_map/out_projection/pallas_call | solution.py:437

commit v4 on v3

--- a/solution.py
+++ b/solution.py
@@ -37,7 +37,6 @@
 
 def stage_plan(n_grp, rows):
     half, near = PORTAL // 2, TILE // 2
-    far = near // 2
     late = (n_grp - 2, n_grp - 1)
     early = range(1, n_grp - 2)
 
@@ -54,9 +53,11 @@
     return [
         portals([o for o in early if o not in odd], 0, PORTAL),
         portals(odd[:-1], 0, PORTAL) + halo(0, near)[:1],
-        halo(0, near)[1:] + portals(late, 0, half),
-        portals(odd[-1:], 0, PORTAL) + halo(near, far),
-        portals(late, half, half) + halo(near + far, far),
+        portals(odd[-1:], 0, PORTAL)
+        + halo(near, near)[:1]
+        + portals(late, 0, half)
+        + halo(0, near)[1:],
+        portals(late, half, half) + halo(near, near)[1:],
     ]
 
 
@@ -344,14 +345,14 @@
         ready(offset - 1)
     send([("portal", offset) for offset in range(n_grp - 2, n_grp)])
 
+    loads[2].wait()
+    loads[3].wait()
+    run_stage(xn.at[pl.ds(0, rows)], biases[0], True, False)
     @pl.when(rng == 0)
     def _send_round():
         ready(n_grp)
         send([("above", None)])
 
-    loads[2].wait()
-    loads[3].wait()
-    run_stage(xn.at[pl.ds(0, rows)], biases[0], True, False)
     place = rows
     for number, buffer in enumerate(landed):
         arrived(number)

time: 22.4 us -> 21.8 us (0.973)
  Pallas kernels: 21.5 us -> 20.9 us
    pallas_call x1, Pallas kernels: 20.1 us -> 19.5 us  [local(): pl.pallas_call(functools.partial(kernel, n_grp, n_rng, plan), out_shape=(...]
where the time goes in v4:
time: 21.8 us; the launch traced here: 21.6 us
  Pallas kernels  20.9 us (96%)
  between operations  0.66 us (3%)
    pallas_call x1, Pallas kernels, local(): pl.pallas_call(functools.partial(kernel, n_grp, n_rng, plan), out_shape=(...  19.5 us
    pallas_call x1, Pallas kernels, local(): pl.pallas_call(project_kernel, out_shape=jax.ShapeDtypeStruct((rows, widt...  1.46 us

profile of v4, /device:TPU:0, one launch (start us, length us, event | category | flops | bytes accessed | tf_op | source)
XLA Modules:
  0.0 21.6 jit_solution(16398706192500462647)
XLA Ops:
  0.7 19.5 %graph_attention.1 = (bf16[256,1024]{1,0:T(8,128)(2,1)S(1)}, bf16[256,1024]{1,0:T(8,128)(2,1)S(1)}, bf16[1024,1024]{1,0:T(8,128)(2,1)S(1)}) custom-call(bf16[256,1024]{1,0:T(8,128)(2,1)} %refs_0_.1, bf16[1024,1024]{1,0:T(8,128)(2,1)} %refs_1_.1, bf16[1024,1024]{1,0:T(8,128)(2,1)} %refs_2_.1, bf16[1024,1024]{1,0:T(8,128)(2,1)} %refs_3_.1, ...), custom_call_target="tpu_custom_call" | custom-call | tf_op jit(solution)/shard_map/graph_attention/pallas_call | solution.py:406
  20.1 1.5 %out_projection.1 = bf16[256,1024]{1,0:T(8,128)(2,1)} custom-call(bf16[256,1024]{1,0:T(8,128)(2,1)S(1)} %get-tuple-element.8.att_ref, bf16[256,1024]{1,0:T(8,128)(2,1)S(1)} %get-tuple-element.9.x_ref, bf16[1024,1024]{1,0:T(8,128)(2,1)S(1)} %get-tuple-element.10.wo_ref), custom_call_target="tpu_custom_call" | custom-call | tf_op jit(solution)/shard_map/out_projection/pallas_call | solution.py:438

commit v5 on v4

--- a/solution.py
+++ b/solution.py
@@ -377,17 +377,13 @@
 
 def project_kernel(att_ref, x_ref, wo_ref, out_hbm, out_v, sem):
     width = out_v.shape[1]
-    block = width // 4
-    copies = []
-    for part in range(4):
+    block = width // 2
+    for part in range(2):
         cols = slice(part * block, (part + 1) * block)
         mixed = jnp.dot(att_ref[...], wo_ref[:, cols], preferred_element_type=F32)
         out_v[:, cols] = (x_ref[:, cols].astype(F32) + mixed).astype(BF16)
-        copy = pltpu.make_async_copy(out_v.at[:, cols], out_hbm.at[:, cols], sem.at[part])
-        copy.start()
-        copies.append(copy)
-    for copy in copies:
-        copy.wait()
+        pltpu.make_async_copy(out_v.at[:, cols], out_hbm.at[:, cols], sem.at[0]).start()
+    pltpu.make_async_copy(out_v, out_hbm, sem.at[0]).wait()
 
 
 def local(n_grp, n_rng, features, wq, wk, wv, wo, reach, peers, count, pick):
@@ -440,7 +436,7 @@
         out_shape=jax.ShapeDtypeStruct((rows, width), BF16),
         in_specs=[whole] * 3,
         out_specs=hbm,
-        scratch_shapes=[vmem(rows, width), pltpu.SemaphoreType.DMA((4,))],
+        scratch_shapes=[vmem(rows, width), pltpu.SemaphoreType.DMA((1,))],
         compiler_params=pltpu.CompilerParams(vmem_limit_bytes=VMEM_LIMIT // 4),
         name="out_projection",
     )(att, x, wo)

time: 21.8 us -> 21.7 us (level)
  no operation moved by 1% of the time
where the time goes in v5:
time: 21.7 us; the launch traced here: 21.6 us
  Pallas kernels  20.9 us (96%)
  between operations  0.66 us (3%)
    pallas_call x1, Pallas kernels, local(): pl.pallas_call(functools.partial(kernel, n_grp, n_rng, plan), out_shape=(...  19.5 us
    pallas_call x1, Pallas kernels, local(): pl.pallas_call(project_kernel, out_shape=jax.ShapeDtypeStruct((rows, widt...  1.42 us

profile of v5, /device:TPU:0, one launch (start us, length us, event | category | flops | bytes accessed | tf_op | source)
XLA Modules:
  0.0 21.6 jit_solution(1187246442926010009)
XLA Ops:
  0.7 19.5 %graph_attention.1 = (bf16[256,1024]{1,0:T(8,128)(2,1)S(1)}, bf16[256,1024]{1,0:T(8,128)(2,1)S(1)}, bf16[1024,1024]{1,0:T(8,128)(2,1)S(1)}) custom-call(bf16[256,1024]{1,0:T(8,128)(2,1)} %refs_0_.1, bf16[1024,1024]{1,0:T(8,128)(2,1)} %refs_1_.1, bf16[1024,1024]{1,0:T(8,128)(2,1)} %refs_2_.1, bf16[1024,1024]{1,0:T(8,128)(2,1)} %refs_3_.1, ...), custom_call_target="tpu_custom_call" | custom-call | tf_op jit(solution)/shard_map/graph_attention/pallas_call | solution.py:402
  20.1 1.4 %out_projection.1 = bf16[256,1024]{1,0:T(8,128)(2,1)} custom-call(bf16[256,1024]{1,0:T(8,128)(2,1)S(1)} %get-tuple-element.8.att_ref, bf16[256,1024]{1,0:T(8,128)(2,1)S(1)} %get-tuple-element.9.x_ref, bf16[1024,1024]{1,0:T(8,128)(2,1)S(1)} %get-tuple-element.10.wo_ref), custom_call_target="tpu_custom_call" | custom-call | tf_op jit(solution)/shard_map/out_projection/pallas_call | solution.py:434
